TPU v7x, 32 devices: a 4x4x1 block of a 4x4x8 slice. The times are simulated.
32 devices in a mesh: dp: 1 (over z), emb: 4 (over y), head: 8 (over x, core).
Axes of the slice: x: 4, y: 4, z: 1, core: 2. Of those that a mesh axis runs over, the one named last changes fastest.
The devices are a block of a 4x4x8 slice.
Arguments:
- hidden: bfloat16 [32, 256, 6144], P('dp', None, 'emb')
- g_in: bfloat16 [6144], P('emb')
- w_dq: bfloat16 [6144, 1536], P('emb', 'head')
- g_q: bfloat16 [1536], P('head')
- w_dkv: bfloat16 [6144, 512], P('emb', 'head')
- g_kv: bfloat16 [512], P('head')
- w_kr: bfloat16 [6144, 64], P('emb')
- w_uq: bfloat16 [1536, 64, 192], P(None, 'head')
- w_uk: bfloat16 [512, 64, 128], P(None, 'head')
- w_uv: bfloat16 [512, 64, 128], P(None, 'head')
- w_o: bfloat16 [64, 128, 6144], P('head', None, 'emb')
Outputs:
- output 1: bfloat16 [32, 256, 6144], P('dp', None, 'emb')
- output 2: bfloat16 [32, 256, 512], P('dp', None, 'head')
- output 3: bfloat16 [32, 256, 64], P('dp')
All inputs are finite; a program needn't handle non-finite values.
Results may differ from a plain program's by a relative error of at most 0.02.
Values are sent between devices in bfloat16 or wider.
A program may use at most 768 MiB of HBM per device.

v0:
```python
import math
import jax
import jax.numpy as jnp
from jax import lax
from jax.sharding import PartitionSpec as P

ROPE_BASE = 10000.0
NORM_EPS = 1.0e-6
MSCALE = 0.1 * math.log(40.0) + 1.0


def split_norm(latent, gain_vec, full_width, axis_name):
    wide_vals = latent.astype(jnp.float32)
    sq_sum = lax.psum(jnp.sum(wide_vals * wide_vals, axis=-1, keepdims=True), axis_name)
    return (wide_vals * lax.rsqrt(sq_sum / full_width + NORM_EPS) * gain_vec.astype(jnp.float32)).astype(jnp.bfloat16)


def rope_tables(seq_len, rope_dim):
    half_dim = rope_dim // 2
    inv_freq = ROPE_BASE ** (-2.0 * jnp.arange(half_dim, dtype=jnp.float32) / rope_dim)
    angles = jnp.arange(seq_len, dtype=jnp.float32)[:, None] * inv_freq[None, :]
    return jnp.cos(angles), jnp.sin(angles)


def rotate(values, cos_t, sin_t):
    half_dim = values.shape[-1] // 2
    front_half = values[..., :half_dim]
    back_half = values[..., half_dim:]
    return jnp.concatenate([front_half * cos_t - back_half * sin_t, front_half * sin_t + back_half * cos_t], axis=-1)


def causal_attention(q_nope, q_pe, k_nope, k_pe, v_heads, soft_scale):
    seq_len = q_nope.shape[1]
    q_block = min(seq_len, 128)
    key_pos = jnp.arange(seq_len)

    def attend_block(blk_idx):
        q_start = blk_idx * q_block
        qn_blk = lax.dynamic_slice_in_dim(q_nope, q_start, q_block, axis=1)
        qp_blk = lax.dynamic_slice_in_dim(q_pe, q_start, q_block, axis=1)
        scores = jnp.einsum("hqd,hkd->hqk", qn_blk, k_nope, preferred_element_type=jnp.float32)
        scores = scores + jnp.einsum("hqr,kr->hqk", qp_blk, k_pe, preferred_element_type=jnp.float32)
        q_pos = q_start + jnp.arange(q_block)
        allowed = key_pos[None, :] <= q_pos[:, None]
        scores = jnp.where(allowed, scores * soft_scale, -jnp.inf)
        attn_prob = jax.nn.softmax(scores, axis=-1).astype(jnp.bfloat16)
        return jnp.einsum("irl,ilw->irw", attn_prob, v_heads, preferred_element_type=jnp.float32).astype(jnp.bfloat16)

    return lax.map(attend_block, jnp.arange(seq_len // q_block))


def solution(mesh):
    emb_count = mesh.shape["emb"]
    in_specs = (P("dp", None, "emb"), P("emb"), P("emb", "head"), P("head"), P("emb", "head"), P("head"), P("emb", None), P(None, "head", None), P(None, "head", None), P(None, "head", None), P("head", None, "emb"))
    out_specs = (P("dp", None, "emb"), P("dp", None, "head"), P("dp", None, None))

    def local_block(hidden, g_in, w_dq, g_q, w_dkv, g_kv, w_kr, w_uq, w_uk, w_uv, w_o):
        seq_len = hidden.shape[1]
        nope_dim = w_uk.shape[2]
        soft_scale = MSCALE * MSCALE / math.sqrt(w_uq.shape[2])
        h_norm = split_norm(hidden, g_in, hidden.shape[2] * emb_count, "emb")
        cq_part = jnp.einsum("btd,dc->btc", h_norm, w_dq, preferred_element_type=jnp.float32).astype(jnp.bfloat16)
        ckv_part = jnp.einsum("btd,dc->btc", h_norm, w_dkv, preferred_element_type=jnp.float32).astype(jnp.bfloat16)
        kr_part = jnp.einsum("btd,dc->btc", h_norm, w_kr, preferred_element_type=jnp.float32).astype(jnp.bfloat16)
        c_q, c_kv, k_raw = lax.psum((cq_part, ckv_part, kr_part), "emb")
        cq_loc = split_norm(c_q, g_q, w_uq.shape[0], "head")
        ckv_loc = split_norm(c_kv, g_kv, w_uk.shape[0], "head")
        cq_full = lax.all_gather(cq_loc, "head", axis=2, tiled=True)
        ckv_full = lax.all_gather(ckv_loc, "head", axis=2, tiled=True)
        cos_t, sin_t = rope_tables(seq_len, w_kr.shape[1])
        k_pe = rotate(k_raw.astype(jnp.float32), cos_t, sin_t).astype(jnp.bfloat16)
        wq_nope = w_uq[:, :, :nope_dim]
        wq_rope = w_uq[:, :, nope_dim:]

        def one_seq(seq_in):
            cq_s, ckv_s, kpe_s = seq_in
            q_nope = jnp.einsum("tc,chk->htk", cq_s, wq_nope, preferred_element_type=jnp.float32).astype(jnp.bfloat16)
            q_raw = jnp.einsum("tc,chk->htk", cq_s, wq_rope, preferred_element_type=jnp.float32).astype(jnp.bfloat16)
            q_pe = rotate(q_raw.astype(jnp.float32), cos_t, sin_t).astype(jnp.bfloat16)
            k_nope = jnp.einsum("tc,chk->htk", ckv_s, w_uk, preferred_element_type=jnp.float32).astype(jnp.bfloat16)
            v_heads = jnp.einsum("tc,chk->htk", ckv_s, w_uv, preferred_element_type=jnp.float32).astype(jnp.bfloat16)
            ctx_blocks = causal_attention(q_nope, q_pe, k_nope, kpe_s, v_heads, soft_scale)
            attn_part = jnp.einsum("nhqv,hvd->nqd", ctx_blocks, w_o, preferred_element_type=jnp.float32).astype(jnp.bfloat16)
            return attn_part.reshape(seq_len, w_o.shape[2])

        attn_part = lax.map(one_seq, (cq_full, ckv_full, k_pe))
        attn_sum = lax.psum(attn_part, "head")
        result = (hidden.astype(jnp.float32) + attn_sum.astype(jnp.float32)).astype(jnp.bfloat16)
        return result, ckv_loc, k_pe

    return jax.shard_map(local_block, mesh=mesh, in_specs=in_specs, out_specs=out_specs, check_vma=False)
```

profile of v0, /device:TPU:97, one launch (start us, length us, event | category | flops | bytes accessed | tf_op | source)
XLA Modules:
  0.0 1465.9 jit_solution(11864536705031879644)
XLA Ops:
  7.3 10.4 fusion.56
  17.6 16.1 %psum.49 = f32[32,256,1]{1,0,2:T(8,128)S(1)} all-reduce(f32[32,256,1]{1,0,2:T(8,128)S(1)} %bitcast.124), channel_id=1, replica_groups=mesh['dp'=1,'emb'=4,'head'=8] {'emb'}, use_global_device_ids=true, to_apply=%region_1.0 | all-reduce | flops 8192 | bytes 65536 | tf_op jit(solution)/shard_map/psum | solution.py:14
  33.8 14.6 fusion.69
  48.4 13.6 fusion.75
  62.0 13.4 fusion.78
  75.7 107.9 %all-reduce.10.cloned.1.call-done = (bf16[32,256,192]{1,2,0:T(8,128)(2,1)}, bf16[32,256,64]{1,2,0:T(8,128)(2,1)}, bf16[32,256,64]{1,2,0:T(8,128)(2,1)}) async-done(((bf16[32,256,192]{1,2,0:T(8,128)(2,1)}, bf16[32,256,64]{1,2,0:T(8,128)(2,1)}, bf16[32,256,64]{1,2,0:T(8,128)(2,1)}), (bf16[32,256,192]{1,2,0:T(8,128)(2,1)}, bf16[32,256,64]{1,2,0:T(8,128)(2,1)}, ...) | async-done | bytes 5242896 | tf_op jit(solution)/shard_map/psum | solution.py:65
  183.6 3.3 fusion.66
  189.1 52.6 %all-reduce.8.cloned.1.call-done = (f32[32,256,1]{1,0,2:T(8,128)}, f32[32,256,1]{1,0,2:T(8,128)}) async-done(((f32[32,256,1]{1,0,2:T(8,128)}, f32[32,256,1]{1,0,2:T(8,128)}), (f32[32,256,1]{1,0,2:T(8,128)}, f32[32,256,1]{1,0,2:T(8,128)})) %all-reduce.8.cloned.1.call-update) | async-done | bytes 65552 | tf_op jit(solution)/shard_map/psum | solution.py:14
  246.1 4.6 fusion.68
  250.9 3.8 slice.18
  257.3 5.0 copy.23
  264.2 29.8 %all-gather.5.cloned.1.call-done = bf16[32,256,512]{1,2,0:T(8,128)(2,1)} async-done(((bf16[32,256,64]{1,2,0:T(8,128)(2,1)}), bf16[32,256,512]{1,2,0:T(8,128)(2,1)}) %all-gather.5.cloned.1.call-update) | async-done | bytes 8388624 | tf_op jit(solution)/shard_map/all_gather | solution.py:69
  293.9 120.0 %all-gather.3.cloned.1.call-done = bf16[32,256,1536]{1,2,0:T(8,128)(2,1)} async-done(((bf16[32,256,192]{1,2,0:T(8,128)(2,1)}), bf16[32,256,1536]{1,2,0:T(8,128)(2,1)}) %all-gather.3.cloned.1.call-update) | async-done | bytes 25165840 | tf_op jit(solution)/shard_map/all_gather | solution.py:68
  413.9 760.5 %while.28 = (s32[]{:T(128)}, bf16[32,256,1536]{2,1,0:T(8,128)(2,1)}, bf16[32,256,1536]{1,2,0:T(8,128)(2,1)}, bf16[1536,8,128]{2,1,0:T(8,128)(2,1)}, bf16[1536,8,...) while((s32[]{:T(128)}, ...), condition=%wide.region_14.15_spmd.clone.clone.clone, body=%wide.region_9.14_spmd.clone.clone.clone.sunk | while | flops 2722670080 | bytes 27701836 | solution.py:86
  423.9 9.8 while.29
  440.2 3.1 fusion.130
  447.7 9.8 while.29
  464.0 3.1 fusion.130
  471.5 9.8 while.29
  487.8 3.1 fusion.130
  495.2 9.8 while.29
  511.5 3.1 fusion.130
  519.0 9.8 while.29
  535.3 3.1 fusion.130
  542.8 9.8 while.29
  559.0 3.1 fusion.130
  566.5 9.8 while.29
  582.8 3.1 fusion.130
  590.3 9.8 while.29
  614.1 9.8 while.29
  630.3 3.1 fusion.130
  637.8 9.8 while.29
  661.6 9.8 while.29
  677.9 3.1 fusion.130
  685.4 9.8 while.29
  709.1 9.8 while.29
  725.4 3.1 fusion.130
  732.9 9.8 while.29
  756.6 9.8 while.29
  772.9 3.1 fusion.130
  780.4 9.8 while.29
  804.2 9.8 while.29
  820.5 3.1 fusion.130
  827.9 9.8 while.29
  851.7 9.8 while.29
  868.0 3.1 fusion.130
  875.5 9.8 while.29
  891.7 3.1 fusion.130
  899.2 9.8 while.29
  915.5 3.1 fusion.130
  923.0 9.8 while.29
  939.3 3.1 fusion.130
  946.8 9.8 while.29
  970.5 9.8 while.29
  994.3 9.8 while.29
  1018.0 9.8 while.29
  1041.8 9.8 while.29
  1065.6 9.8 while.29
  1089.3 9.8 while.29
  1113.1 9.8 while.29
  1136.9 9.8 while.29
  1160.6 9.8 while.29
  1174.5 256.9 %all-reduce.6.cloned.1.call-done = bf16[32,256,1536]{2,1,0:T(8,128)(2,1)} async-done(((bf16[32,256,1536]{2,1,0:T(8,128)(2,1)}), bf16[32,256,1536]{2,1,0:T(8,128)(2,1)}) %all-reduce.6.cloned.1.call-update) | async-done | bytes 25165840 | tf_op jit(solution)/shard_map/psum | solution.py:87
  1431.4 28.0 %fusion.59 = bf16[32,256,1536]{2,1,0:T(8,128)(2,1)} fusion(bf16[32,256,1536]{2,1,0:T(8,128)(2,1)} %param.15, bf16[32,256,1536]{2,1,0:T(8,128)(2,1)} %all-reduce.6.cloned.1.call-done), kind=kLoop, calls=%fused_computation.65 | loop fusion | flops 50331648 | bytes 75497472 | tf_op jit(solution)/shard_map/convert_element_type | solution.py:88
  (889 shorter events, 680.9 us)
Async XLA Ops:
  7.2 26.6 %copy-start = (bf16[1536,192]{0,1:T(8,128)(2,1)S(1)}, bf16[1536,192]{0,1:T(8,128)(2,1)}, u32[]{:S(2)}) copy-start(bf16[1536,192]{0,1:T(8,128)(2,1)} %param.17) | copy-start | bytes 1769476
  7.2 26.6 %copy-start.3 = (bf16[1536]{0:T(1024)(128)(2,1)S(1)}, bf16[1536]{0:T(1024)(128)(2,1)}, u32[]{:S(2)}) copy-start(bf16[1536]{0:T(1024)(128)(2,1)} %param.16) | copy-start | bytes 9220
  7.2 176.4 %all-reduce.10.cloned.1.call-start = ((), (), s32[]{:S(2)}) async-start(), calls=%async_computation.4 | async-start | bytes 10485760 | tf_op jit(solution)/shard_map/psum | solution.py:65
  33.8 14.6 copy-start.4
  48.4 13.6 copy-start.5
  62.0 127.1 %copy-start.6 = (bf16[64]{0:T(256)(128)(2,1)S(1)}, bf16[64]{0:T(256)(128)(2,1)}, u32[]{:S(2)}) copy-start(bf16[64]{0:T(256)(128)(2,1)} %param.20) | copy-start | bytes 388
  62.0 183.3 %copy-start.7 = (bf16[192]{0:T(256)(128)(2,1)S(1)}, bf16[192]{0:T(256)(128)(2,1)}, u32[]{:S(2)}) copy-start(bf16[192]{0:T(256)(128)(2,1)} %param.18) | copy-start | bytes 1156
  75.4 166.3 %all-reduce.8.cloned.1.call-start = ((), (), s32[]{:S(2)}) async-start(), calls=%async_computation.3 | async-start | bytes 131072 | tf_op jit(solution)/shard_map/psum | solution.py:14
  183.6 78.9 %copy-start.2 = (bf16[32,256,64]{1,2,0:T(8,128)(2,1)S(1)}, bf16[32,256,64]{1,2,0:T(8,128)(2,1)}, u32[]{:S(2)}) copy-start(bf16[32,256,64]{1,2,0:T(8,128)(2,1)} %get-tuple-element.280) | copy-start | bytes 3145732
  189.0 104.9 %all-gather.5.cloned.1.call-start = ((), (), s32[]{:S(2)}) async-start(), calls=%async_computation.1 | async-start | bytes 9437184 | tf_op jit(solution)/shard_map/all_gather | solution.py:69
  245.2 168.7 %all-gather.3.cloned.1.call-start = ((), (), s32[]{:S(2)}) async-start(), calls=%async_computation | async-start | bytes 28311552 | tf_op jit(solution)/shard_map/all_gather | solution.py:68
  250.8 1180.6 %all-reduce.6.cloned.1.call-start = ((), (), s32[]{:S(2)}) async-start(), calls=%async_computation.2 | async-start | bytes 50331648 | tf_op jit(solution)/shard_map/psum | solution.py:87
  1174.4 284.9 %copy-start.1 = (bf16[1536,192]{0,1:T(8,128)(2,1)S(1)}, bf16[1536,192]{0,1:T(8,128)(2,1)}, u32[]{:S(2)}) copy-start(bf16[1536,192]{0,1:T(8,128)(2,1)} %param.17) | copy-start | bytes 1769476
Sparse Core Ops, SparseCore 0:
  75.6 108.0 all-reduce.9
  189.2 52.5 all-reduce.7
  245.4 48.5 all-gather.4
  295.4 118.4 all-gather.2
  1174.6 256.7 all-reduce.5
where the time goes:
time: 1470 us
  matrix products  630 us (43%)
  waiting for transfers between devices  567 us (39%)
  local copies, waits for them, and re-layouts  103 us (7%)
  other arithmetic  93.8 us (6%)
  loops' own time  41 us (3%)
  blocking collectives  16.1 us (1%)
    psum x1, waiting for transfers between devices, local_block(): attn_sum = lax.psum(attn_part, 'head')  257 us
    dot_general x64, matrix products, attend_block(): jnp.einsum('irl,ilw->irw', attn_prob, v_heads, preferred_element_type=jnp...  168 us
    all_gather x1, waiting for transfers between devices, local_block(): cq_full = lax.all_gather(cq_loc, 'head', axis=2, tiled=True)  120 us
    psum x1, waiting for transfers between devices, local_block(): c_q, c_kv, k_raw = lax.psum((cq_part, ckv_part, kr_part), 'emb')  108 us
    dot_general x32, matrix products, one_seq(): jnp.einsum('tc,chk->htk', cq_s, wq_nope, preferred_element_type=jnp.float32)  100 us
    dot_general x32, matrix products, one_seq(): jnp.einsum('nhqv,hvd->nqd', ctx_blocks, w_o, preferred_element_type=jnp.f...  97.1 us
    while x32, matrix products  69.5 us
    dot_general x32, matrix products, one_seq(): jnp.einsum('tc,chk->htk', ckv_s, w_uk, preferred_element_type=jnp.float32)  56.8 us
  transfers between devices with their start and end apart: 5, of which 5 were waited for; matrix products, arithmetic and copies ran while one was open for 1% of the time, Pallas kernels for 0%

commit v1 on v0

v1 whole, which is shorter than its diff:
```python
import functools
import math

import jax
import jax.numpy as jnp
from jax import lax
from jax.experimental import pallas as pl
from jax.experimental.pallas import tpu as pltpu
from jax.sharding import PartitionSpec as P

ROPE_BASE = 10000.0
NORM_EPS = 1.0e-6
MSCALE = 0.1 * math.log(40.0) + 1.0
LOG2E = math.log2(math.e)
F32 = jnp.float32
BF16 = jnp.bfloat16


def rope_rows(seq_len, rope_dim):
    half = rope_dim // 2
    inv_freq = ROPE_BASE ** (-2.0 * jnp.arange(half, dtype=F32) / rope_dim)
    angles = jnp.arange(seq_len, dtype=F32)[:, None] * inv_freq[None, :]
    c, s = jnp.cos(angles), jnp.sin(angles)
    return jnp.concatenate([c, c, c, c], -1), jnp.concatenate([-s, s, -s, s], -1)


def attn_kernel(heads, rope, cq_w, scale, lat_ref, own_ref, wq_ref, wk_ref, wv_ref, gown_ref, cos_ref, sin_ref, o_ref, small_ref):
    parts, width = lat_ref.shape[0], lat_ref.shape[3]
    seq = cos_ref.shape[0]
    nope = wk_ref.shape[1] // heads
    hd = nope + rope
    half = seq // 2
    pieces = [lat_ref[j, 0, :seq] for j in range(parts)]
    gains = [jnp.concatenate([lat_ref[j, 0, seq : seq + 1, width // 2 :], lat_ref[j, 0, seq + 1 : seq + 2, width // 2 :]], axis=-1).astype(F32) for j in range(parts)]
    gq = jnp.concatenate([g[:, :cq_w] for g in gains], axis=-1)
    gkv = jnp.concatenate([g[:, cq_w:] for g in gains], axis=-1)
    cq = jnp.concatenate([p[:, :cq_w] for p in pieces], axis=-1).astype(F32)
    ckv = jnp.concatenate([p[:, cq_w:] for p in pieces], axis=-1).astype(F32)
    rq = lax.rsqrt(jnp.mean(cq * cq, axis=-1, keepdims=True) + NORM_EPS)
    rkv = lax.rsqrt(jnp.mean(ckv * ckv, axis=-1, keepdims=True) + NORM_EPS)
    cqn = (cq * rq * gq).astype(BF16)
    ckvn = (ckv * rkv * gkv).astype(BF16)

    lane = lax.broadcasted_iota(jnp.int32, (seq, 2 * rope), 1)
    first = (lane % rope) < (rope // 2)
    cos_t, sin_t = cos_ref[...], sin_ref[...]

    def rot(x):
        swapped = jnp.where(first, pltpu.roll(x, 2 * rope - rope // 2, 1), pltpu.roll(x, rope // 2, 1))
        return (x * cos_t + swapped * sin_t).astype(BF16)

    own = own_ref[0, :seq].astype(F32)
    own_ckv = (own[:, cq_w:] * rkv * gown_ref[...].astype(F32)).astype(BF16)
    kpe2 = rot(jnp.concatenate([lat_ref[j, 0, seq:, : width // 2] for j in range(parts)], axis=0).astype(F32))
    small_ref[0] = jnp.concatenate([own_ckv, kpe2[:, :rope]], axis=-1)
    zero = jnp.zeros_like(kpe2)
    kpe = (jnp.where(lane < rope, kpe2, zero), jnp.where(lane >= rope, kpe2, zero))

    nt = (((1,), (1,)), ((), ()))

    def q_cols(first_col, count, ns):
        rows_t = jnp.concatenate([wq_ref[hd * n + first_col : hd * n + first_col + count, :] for n in ns], axis=0)
        return lax.dot_general(cqn, rows_t, nt, preferred_element_type=F32).astype(BF16)

    qn = [q_cols(0, nope, (n, n + 1)) for n in range(0, heads, 2)]
    qr = [q_cols(nope, rope, range(n, n + 4)).astype(F32) for n in range(0, heads, 4)]
    kn = jnp.dot(ckvn, wk_ref[...], preferred_element_type=F32).astype(BF16)
    vv = jnp.dot(ckvn, wv_ref[...], preferred_element_type=F32).astype(BF16)

    row = lax.broadcasted_iota(jnp.int32, (half, half), 0)
    col = lax.broadcasted_iota(jnp.int32, (half, half), 1)
    tri = col <= row
    c2 = scale * LOG2E
    for n in range(heads):
        if n % 2 == 0:
            qpe = rot(qr[n // 4][:, rope * (n % 4) : rope * (n % 4 + 2)])
        q = jnp.concatenate([qn[n // 2][:, nope * (n % 2) : nope * (n % 2 + 1)], qpe], axis=-1)
        k = jnp.concatenate([kn[:, nope * n : nope * (n + 1)], kpe[n % 2]], axis=-1)
        v = vv[:, nope * n : nope * (n + 1)]
        s0 = lax.dot_general(q[:half], k[:half], nt, preferred_element_type=F32)
        s1 = lax.dot_general(q[half:], k, nt, preferred_element_type=F32)
        s0 = jnp.where(tri, s0 * c2, -jnp.inf)
        e0 = jnp.exp2(s0 - jnp.max(s0, axis=-1, keepdims=True))
        p0 = (e0 / jnp.sum(e0, axis=-1, keepdims=True)).astype(BF16)
        sa = s1[:, :half] * c2
        sb = jnp.where(tri, s1[:, half:] * c2, -jnp.inf)
        m1 = jnp.max(jnp.maximum(sa, sb), axis=-1, keepdims=True)
        ea, eb = jnp.exp2(sa - m1), jnp.exp2(sb - m1)
        inv = 1.0 / jnp.sum(ea + eb, axis=-1, keepdims=True)
        p1 = jnp.concatenate([(ea * inv).astype(BF16), (eb * inv).astype(BF16)], axis=-1)
        o_ref[0, :half, nope * n : nope * (n + 1)] = jnp.dot(p0, v[:half], preferred_element_type=F32).astype(BF16)
        o_ref[0, half:, nope * n : nope * (n + 1)] = jnp.dot(p1, v, preferred_element_type=F32).astype(BF16)


def attention(lat, own, weights, gown, tables, scale, heads, rope, cq_w):
    parts, nseq, ext, width = lat.shape
    seq = tables[0].shape[0]
    whole = lambda a: pl.BlockSpec(a.shape, lambda s: (0,) * a.ndim)
    o_w = weights[2].shape[1]
    flops = 2 * nseq * seq * sum(w.shape[0] * w.shape[1] for w in weights) + 4 * nseq * heads * seq * seq * 256
    return pl.pallas_call(
        functools.partial(attn_kernel, heads, rope, cq_w, scale),
        grid=(nseq,),
        in_specs=[pl.BlockSpec((parts, 1, ext, width), lambda s: (0, s, 0, 0)), pl.BlockSpec((1, ext, width), lambda s: (s, 0, 0))] + [whole(a) for a in (*weights, gown, *tables)],
        out_specs=[pl.BlockSpec((1, seq, o_w), lambda s: (s, 0, 0)), pl.BlockSpec((1, seq, 2 * rope), lambda s: (s, 0, 0))],
        out_shape=[jax.ShapeDtypeStruct((nseq, seq, o_w), BF16), jax.ShapeDtypeStruct((nseq, seq, 2 * rope), BF16)],
        compiler_params=pltpu.CompilerParams(vmem_limit_bytes=60 * 1024 * 1024),
        cost_estimate=pl.CostEstimate(flops=flops, bytes_accessed=lat.size * 2, transcendentals=0),
        name="mla_attention",
    )(lat, own, *weights, gown, *tables)


MESH = pl.DeviceIdType.MESH


def tail_kernel(rows, o_hbm, w_ref, h_hbm, out_hbm, obuf, pall, precv, r2p, r2m, r1p, r1m, fin, hbuf, osend, orecv, hsend, hrecv, loc, s_snd, s_rcv, x_snd, x_rcv, g_snd, g_rcv, q_snd, q_rcv):
    y, j = lax.axis_index("emb"), lax.axis_index("head")
    emb, nown, seq, width = out_hbm.shape
    ring = nown // 2
    quarters = seq // rows
    units = emb * quarters
    hr = rows // 2
    x, c = j // 2, j % 2
    x_next, x_prev = (x + 1) % ring, (x + ring - 1) % ring
    x_far = (x + 2) % ring
    y_next, y_prev = (y + 1) % emb, (y + emb - 1) % emb
    to_next, to_prev = {"head": 2 * x_next + c}, {"head": 2 * x_prev + c}
    to_sib = {"head": 2 * x + 1 - c}
    to_up, to_down = {"emb": y_next}, {"emb": y_prev}
    half_k = nown // 2

    barrier = pltpu.get_barrier_semaphore()
    for dev in (to_next, to_prev, to_sib, to_up, to_down):
        pl.semaphore_signal(barrier, inc=1, device_id=dev, device_id_type=MESH)

    def remote(src, dst, ssem, rsem, dev):
        return pltpu.make_async_remote_copy(src_ref=src, dst_ref=dst, send_sem=ssem, recv_sem=rsem, device_id=dev, device_id_type=MESH)

    def own_in(r):
        return pltpu.make_async_copy(o_hbm.at[:, pl.ds(r * rows, rows), :], obuf.at[r], loc.at[r])

    h_in = pltpu.make_async_copy(h_hbm.at[:, j], hbuf, loc.at[quarters])
    for r in range(quarters):
        own_in(r).start()
    h_in.start()
    pl.semaphore_wait(barrier, 5)

    def o_down(r):
        return remote(obuf.at[r], obuf.at[quarters + 3 * r], osend.at[2 * r], orecv.at[2 * r], to_down)

    def o_up(r):
        return remote(obuf.at[r], obuf.at[quarters + 3 * r + 1], osend.at[2 * r + 1], orecv.at[2 * r + 1], to_up)

    def o_half_up(r):
        return remote(obuf.at[quarters + 3 * r + 1, pl.ds(0, half_k)], obuf.at[quarters + 3 * r + 2, pl.ds(0, half_k)], hsend.at[2 * r], hrecv.at[2 * r], to_up)

    def o_half_down(r):
        return remote(obuf.at[quarters + 3 * r, pl.ds(half_k, half_k)], obuf.at[quarters + 3 * r + 2, pl.ds(half_k, half_k)], hsend.at[2 * r + 1], hrecv.at[2 * r + 1], to_down)

    for r in range(quarters):
        own_in(r).wait()
        o_down(r).start()
        o_up(r).start()
    h_in.wait()

    def place(u):
        v = u - quarters
        w = v % 3
        off = 1 + 2 * w - 3 * (w // 2)
        is_own = u < quarters
        yy = jnp.where(is_own, y, (y + off) % emb)
        return yy, jnp.where(is_own, u, v // 3)

    def spot(ref, u, owner, lo, n):
        yy, r = place(u)
        return ref.at[yy, owner, pl.ds(r * rows + lo, n), :]

    def d2d(u):
        return remote(pall.at[u % 4, :, 1 - c], precv.at[u], s_snd.at[u], s_rcv.at[u], to_sib)

    def far_next(u):
        return remote(pall.at[u % 4, x_far, c, pl.ds(0, hr)], r2p.at[u], x_snd.at[0, u], x_rcv.at[0, u], to_next)

    def far_prev(u):
        return remote(pall.at[u % 4, x_far, c, pl.ds(hr, hr)], r2m.at[u], x_snd.at[1, u], x_rcv.at[1, u], to_prev)

    def near_next(u):
        return remote(pall.at[u % 4, x_next, c], r1p.at[u], x_snd.at[2, u], x_rcv.at[2, u], to_next)

    def near_prev(u):
        return remote(pall.at[u % 4, x_prev, c], r1m.at[u], x_snd.at[3, u], x_rcv.at[3, u], to_prev)

    def fin_local(u):
        return pltpu.make_async_copy(fin.at[u], spot(out_hbm, u, j, 0, rows), g_snd.at[3, u])

    def gather(u, owner, k, dev):
        return remote(fin.at[u], spot(out_hbm, u, owner, 0, rows), g_snd.at[k, u], g_rcv.at[k, u], dev)

    def relay(u, owner, lo, n, k, dev):
        return remote(spot(out_hbm, u, owner, lo, n), spot(out_hbm, u, owner, lo, n), q_snd.at[k, u], q_rcv.at[k, u], dev)

    own_next, own_prev, own_far = 2 * x_next + c, 2 * x_prev + c, 2 * x_far + c
    sib = 1 - 2 * c

    def stage_a(u):
        @pl.when(u >= quarters)
        def _():
            v = u - quarters
            r = v // 3

            @pl.when(v % 3 == 0)
            def _():
                o_down(r).wait_recv()
                o_half_down(r).start()

            @pl.when(v % 3 == 1)
            def _():
                o_up(r).wait_recv()
                o_half_up(r).start()

            @pl.when(v % 3 == 2)
            def _():
                o_half_up(r).wait_recv()
                o_half_down(r).wait_recv()

        @pl.when(u >= 4)
        def _():
            for cp in (d2d, far_next, far_prev, near_next, near_prev):
                cp(u - 4).wait_send()

        lhs = obuf[u].reshape(nown * rows, obuf.shape[3])
        tile = width // 3
        for n in range(3):
            res = jnp.dot(lhs, w_ref[:, n * tile : (n + 1) * tile], preferred_element_type=F32)
            pall[u % 4, :, :, :, n * tile : (n + 1) * tile] = res.astype(BF16).reshape(ring, 2, rows, tile)
        d2d(u).start()

    def stage_b(u):
        d2d(u).wait_recv()
        for i in range(ring):
            pall[u % 4, i, c] = (pall[u % 4, i, c].astype(F32) + precv[u, i].astype(F32)).astype(BF16)
        far_next(u).start()
        far_prev(u).start()

    def stage_c(u):
        far_next(u).wait_recv()
        pall[u % 4, x_next, c, pl.ds(0, hr)] = (pall[u % 4, x_next, c, pl.ds(0, hr)].astype(F32) + r2p[u].astype(F32)).astype(BF16)
        near_next(u).start()
        far_prev(u).wait_recv()
        pall[u % 4, x_prev, c, pl.ds(hr, hr)] = (pall[u % 4, x_prev, c, pl.ds(hr, hr)].astype(F32) + r2m[u].astype(F32)).astype(BF16)
        near_prev(u).start()

    def stage_d(u):
        near_next(u).wait_recv()
        near_prev(u).wait_recv()
        yy, r = place(u)
        total = pall[u % 4, x, c].astype(F32) + r1p[u].astype(F32) + r1m[u].astype(F32)
        fin[u] = (hbuf[yy, pl.ds(r * rows, rows)].astype(F32) + total).astype(BF16)
        gather(u, j, 0, to_next).start()
        gather(u, j, 1, to_prev).start()
        gather(u, j, 2, to_sib).start()
        fin_local(u).start()

    def stage_e(u):
        gather(u, own_prev, 0, to_next).wait_recv()
        relay(u, own_prev, 0, hr, 0, to_next).start()
        relay(u, own_prev, 0, rows, 2, to_sib).start()
        gather(u, own_next, 1, to_prev).wait_recv()
        relay(u, own_next, hr, hr, 1, to_prev).start()
        relay(u, own_next, 0, rows, 3, to_sib).start()

    def stage_g(u):
        relay(u, own_far, 0, hr, 0, to_next).wait_recv()
        relay(u, own_far, 0, hr, 4, to_sib).start()
        relay(u, own_far, hr, hr, 1, to_prev).wait_recv()
        relay(u, own_far, hr, hr, 5, to_sib).start()

    stages = (stage_a, stage_b, stage_c, stage_d, stage_e, stage_g)

    @pl.loop(0, units + len(stages) - 1)
    def _(t):
        for lag, stage in enumerate(stages):

            @pl.when((t >= lag) & (t < units + lag))
            def _():
                stage(t - lag)

    @pl.loop(0, units)
    def _(u):
        @pl.when(u >= units - 4)
        def _():
            for cp in (d2d, far_next, far_prev, near_next, near_prev):
                cp(u).wait_send()

        fin_local(u).wait()
        gather(u, j, 0, to_next).wait_send()
        gather(u, j, 1, to_prev).wait_send()
        gather(u, j, 2, to_sib).wait_send()
        relay(u, own_prev, 0, hr, 0, to_next).wait_send()
        relay(u, own_next, hr, hr, 1, to_prev).wait_send()
        relay(u, own_prev, 0, rows, 2, to_sib).wait_send()
        relay(u, own_next, 0, rows, 3, to_sib).wait_send()
        relay(u, own_far, 0, hr, 4, to_sib).wait_send()
        relay(u, own_far, hr, hr, 5, to_sib).wait_send()
        gather(u, j + sib, 2, to_sib).wait_recv()
        relay(u, own_prev + sib, 0, rows, 2, to_sib).wait_recv()
        relay(u, own_next + sib, 0, rows, 3, to_sib).wait_recv()
        relay(u, own_far + sib, 0, hr, 4, to_sib).wait_recv()
        relay(u, own_far + sib, hr, hr, 5, to_sib).wait_recv()

    for r in range(quarters):
        o_down(r).wait_send()
        o_up(r).wait_send()
        o_half_up(r).wait_send()
        o_half_down(r).wait_send()


def tail(o, w_o, hidden, emb):
    nseq, seq, depth = o.shape
    batch, _, width = hidden.shape
    assert batch == emb * nseq and emb == 4 and nseq == 8
    rows = seq // 4
    units = 4 * emb
    dma = pltpu.SemaphoreType.DMA
    h4 = hidden.reshape(emb, nseq, seq, width)
    out = pl.pallas_call(
        functools.partial(tail_kernel, rows),
        out_shape=jax.ShapeDtypeStruct(h4.shape, BF16),
        in_specs=[pl.BlockSpec(memory_space=pl.ANY), pl.BlockSpec(memory_space=pltpu.VMEM), pl.BlockSpec(memory_space=pl.ANY)],
        out_specs=pl.BlockSpec(memory_space=pl.ANY),
        scratch_shapes=[
            pltpu.VMEM((units, nseq, rows, depth), BF16),
            pltpu.VMEM((4, nseq // 2, 2, rows, width), BF16),
            pltpu.VMEM((units, nseq // 2, rows, width), BF16),
            pltpu.VMEM((units, rows // 2, width), BF16),
            pltpu.VMEM((units, rows // 2, width), BF16),
            pltpu.VMEM((units, rows, width), BF16),
            pltpu.VMEM((units, rows, width), BF16),
            pltpu.VMEM((units, rows, width), BF16),
            pltpu.VMEM((emb, seq, width), BF16),
            dma((8,)), dma((8,)), dma((8,)), dma((8,)), dma((5,)),
            dma((units,)), dma((units,)),
            dma((4, units)), dma((4, units)),
            dma((4, units)), dma((3, units)),
            dma((6, units)), dma((6, units)),
        ],
        compiler_params=pltpu.CompilerParams(collective_id=0, has_side_effects=True, vmem_limit_bytes=63 * 1024 * 1024),
        cost_estimate=pl.CostEstimate(flops=2 * batch * seq * depth * width, bytes_accessed=4 * batch * seq * width, transcendentals=0),
        name="mla_tail",
    )(o, w_o, h4)
    return out.reshape(batch, seq, width)


def latent_kernel(cq_w, ckv_w, kr_w, full_width, h_hbm, g_ref, w_ref, gains_ref, lat_hbm, own_hbm, hbuf, ssum, peers, pall, r2p, r2m, r1p, r1m, fin, h_sem, p_snd, p_rcv, y_snd, y_rcv, g_snd, g_rcv, q_snd, q_rcv):
    y, j = lax.axis_index("emb"), lax.axis_index("head")
    emb, nown, seq, width = h_hbm.shape
    units = nown
    ring = nown // 2
    ext = fin.shape[1]
    sub = seq // nown
    lat_w = cq_w + ckv_w
    hr = ext // 2
    x, c = j // 2, j % 2
    x_next, x_prev, x_far = (x + 1) % ring, (x + ring - 1) % ring, (x + 2) % ring
    y_next, y_prev, y_far = (y + 1) % emb, (y + emb - 1) % emb, (y + 2) % emb
    to_next, to_prev = {"head": 2 * x_next + c}, {"head": 2 * x_prev + c}
    to_sib = {"head": 2 * x + 1 - c}
    to_up, to_down, to_far = {"emb": y_next}, {"emb": y_prev}, {"emb": y_far}

    barrier = pltpu.get_barrier_semaphore()
    for dev in (to_next, to_prev, to_sib, to_up, to_down, to_far):
        pl.semaphore_signal(barrier, inc=1, device_id=dev, device_id_type=MESH)

    def remote(src, dst, ssem, rsem, dev):
        return pltpu.make_async_remote_copy(src_ref=src, dst_ref=dst, send_sem=ssem, recv_sem=rsem, device_id=dev, device_id_type=MESH)

    def h_in(s):
        return pltpu.make_async_copy(h_hbm.at[s // nown, s % nown], hbuf.at[s], h_sem.at[s])

    @pl.loop(0, emb * nown)
    def _(s):
        h_in(s).start()

    @pl.loop(0, emb * nown)
    def _(s):
        h_in(s).wait()
        acc = jnp.zeros((seq, 128), F32)
        for n in range(width // 128):
            piece = hbuf[s, :, 128 * n : 128 * (n + 1)].astype(F32)
            acc += piece * piece
        ssum[s // 8, pl.ds(s % 8, 1), :] = jnp.sum(acc.T, axis=0, keepdims=True)

    pl.semaphore_wait(barrier, 6)

    def stat(k, dev):
        return remote(ssum, peers.at[k], p_snd.at[k], p_rcv.at[k], dev)

    stats = (stat(0, to_up), stat(1, to_down), stat(2, to_far))
    for cp in stats:
        cp.start()
    for cp in stats:
        cp.wait_recv()

    def far_up(u):
        return remote(pall.at[u, y_far, pl.ds(0, hr)], r2p.at[u], y_snd.at[0, u], y_rcv.at[0, u], to_up)

    def far_down(u):
        return remote(pall.at[u, y_far, pl.ds(hr, hr)], r2m.at[u], y_snd.at[1, u], y_rcv.at[1, u], to_down)

    def near_up(u):
        return remote(pall.at[u, y_next], r1p.at[u], y_snd.at[2, u], y_rcv.at[2, u], to_up)

    def near_down(u):
        return remote(pall.at[u, y_prev], r1m.at[u], y_snd.at[3, u], y_rcv.at[3, u], to_down)

    def local(u, k):
        return pltpu.make_async_copy(fin.at[u], own_hbm.at[u] if k else lat_hbm.at[j, u], g_snd.at[3 + k, u])

    def gather(u, owner, k, dev):
        return remote(fin.at[u], lat_hbm.at[owner, u], g_snd.at[k, u], g_rcv.at[k, u], dev)

    def relay(u, owner, lo, n, k, dev):
        part = lat_hbm.at[owner, u, pl.ds(lo, n), :]
        return remote(part, part, q_snd.at[k, u], q_rcv.at[k, u], dev)

    own_next, own_prev, own_far = 2 * x_next + c, 2 * x_prev + c, 2 * x_far + c
    sib = 1 - 2 * c
    nt = (((1,), (1,)), ((), ()))

    def stage_a(u):
        @pl.loop(0, emb)
        def _(yy):
            s = yy * nown + u
            ss = ssum[s // 8, pl.ds(s % 8, 1), :]
            for k in range(3):
                ss = ss + peers[k, s // 8, pl.ds(s % 8, 1), :]
            r_row = lax.rsqrt(ss / full_width + NORM_EPS)
            r = jnp.broadcast_to(r_row, (128, seq)).T
            hn = []
            for n in range(width // 128):
                piece = hbuf[s, :, 128 * n : 128 * (n + 1)].astype(F32)
                hn.append((piece * r * g_ref[:, 128 * n : 128 * (n + 1)].astype(F32)).astype(BF16))
            hn = jnp.concatenate(hn, axis=-1)
            hbuf[s] = hn
            pall[u, yy, pl.ds(0, seq), :] = lax.dot_general(hn, w_ref[pl.ds(0, lat_w), :], nt, preferred_element_type=F32).astype(BF16)
            mine = hbuf[s, pl.ds(j * sub, sub), :]
            kr = lax.dot_general(mine, w_ref[pl.ds(lat_w, 2 * kr_w), :], nt, preferred_element_type=F32).astype(BF16)
            pall[u, yy, pl.ds(seq, sub), pl.ds(0, 2 * kr_w)] = kr
            pall[u, yy, pl.ds(seq, sub), pl.ds(2 * kr_w, 2 * kr_w)] = jnp.zeros_like(kr)

        far_up(u).start()
        far_down(u).start()

    def stage_b(u):
        far_up(u).wait_recv()
        pall[u, y_next, pl.ds(0, hr)] = (pall[u, y_next, pl.ds(0, hr)].astype(F32) + r2p[u].astype(F32)).astype(BF16)
        near_up(u).start()
        far_down(u).wait_recv()
        pall[u, y_prev, pl.ds(hr, hr)] = (pall[u, y_prev, pl.ds(hr, hr)].astype(F32) + r2m[u].astype(F32)).astype(BF16)
        near_down(u).start()

    def stage_c(u):
        near_up(u).wait_recv()
        near_down(u).wait_recv()
        fin[u] = (pall[u, y].astype(F32) + r1p[u].astype(F32) + r1m[u].astype(F32)).astype(BF16)
        fin[u, pl.ds(seq, sub), pl.ds(2 * kr_w, 2 * kr_w)] = gains_ref[...]
        gather(u, j, 0, to_next).start()
        gather(u, j, 1, to_prev).start()
        gather(u, j, 2, to_sib).start()
        local(u, 0).start()
        local(u, 1).start()

    def stage_d(u):
        gather(u, own_prev, 0, to_next).wait_recv()
        relay(u, own_prev, 0, hr, 0, to_next).start()
        relay(u, own_prev, 0, ext, 2, to_sib).start()
        gather(u, own_next, 1, to_prev).wait_recv()
        relay(u, own_next, hr, hr, 1, to_prev).start()
        relay(u, own_next, 0, ext, 3, to_sib).start()

    def stage_e(u):
        relay(u, own_far, 0, hr, 0, to_next).wait_recv()
        relay(u, own_far, 0, hr, 4, to_sib).start()
        relay(u, own_far, hr, hr, 1, to_prev).wait_recv()
        relay(u, own_far, hr, hr, 5, to_sib).start()

    stages = (stage_a, stage_b, stage_c, stage_d, stage_e)

    @pl.loop(0, units + len(stages) - 1)
    def _(t):
        for lag, stage in enumerate(stages):

            @pl.when((t >= lag) & (t < units + lag))
            def _():
                stage(t - lag)

    @pl.loop(0, units)
    def _(u):
        for cp in (far_up, far_down, near_up, near_down):
            cp(u).wait_send()
        local(u, 0).wait()
        local(u, 1).wait()
        gather(u, j, 0, to_next).wait_send()
        gather(u, j, 1, to_prev).wait_send()
        gather(u, j, 2, to_sib).wait_send()
        relay(u, own_prev, 0, hr, 0, to_next).wait_send()
        relay(u, own_next, hr, hr, 1, to_prev).wait_send()
        relay(u, own_prev, 0, ext, 2, to_sib).wait_send()
        relay(u, own_next, 0, ext, 3, to_sib).wait_send()
        relay(u, own_far, 0, hr, 4, to_sib).wait_send()
        relay(u, own_far, hr, hr, 5, to_sib).wait_send()
        gather(u, j + sib, 2, to_sib).wait_recv()
        relay(u, own_prev + sib, 0, ext, 2, to_sib).wait_recv()
        relay(u, own_next + sib, 0, ext, 3, to_sib).wait_recv()
        relay(u, own_far + sib, 0, hr, 4, to_sib).wait_recv()
        relay(u, own_far + sib, hr, hr, 5, to_sib).wait_recv()

    for cp in stats:
        cp.wait_send()


def latents(h4, g_in, w_t, gains, cq_w, ckv_w, kr_w):
    emb, nseq, seq, width = h4.shape
    lat_w = cq_w + ckv_w
    assert emb == 4 and nseq == 8 and lat_w == 4 * kr_w
    ext = seq + seq // nseq
    dma = pltpu.SemaphoreType.DMA
    vm = pl.BlockSpec(memory_space=pltpu.VMEM)
    hbm = pl.BlockSpec(memory_space=pl.ANY)
    return pl.pallas_call(
        functools.partial(latent_kernel, cq_w, ckv_w, kr_w, width * emb),
        out_shape=[jax.ShapeDtypeStruct((nseq, nseq, ext, lat_w), BF16), jax.ShapeDtypeStruct((nseq, ext, lat_w), BF16)],
        in_specs=[hbm, vm, vm, vm],
        out_specs=[hbm, hbm],
        scratch_shapes=[
            pltpu.VMEM((emb * nseq, seq, width), BF16),
            pltpu.VMEM((emb * nseq // 8, 8, seq), F32),
            pltpu.VMEM((3, emb * nseq // 8, 8, seq), F32),
            pltpu.VMEM((nseq, emb, ext, lat_w), BF16),
            pltpu.VMEM((nseq, ext // 2, lat_w), BF16),
            pltpu.VMEM((nseq, ext // 2, lat_w), BF16),
            pltpu.VMEM((nseq, ext, lat_w), BF16),
            pltpu.VMEM((nseq, ext, lat_w), BF16),
            pltpu.VMEM((nseq, ext, lat_w), BF16),
            dma((emb * nseq,)), dma((3,)), dma((3,)),
            dma((4, nseq)), dma((4, nseq)),
            dma((5, nseq)), dma((3, nseq)),
            dma((6, nseq)), dma((6, nseq)),
        ],
        compiler_params=pltpu.CompilerParams(collective_id=1, has_side_effects=True, vmem_limit_bytes=60 * 1024 * 1024),
        cost_estimate=pl.CostEstimate(flops=2 * emb * nseq * seq * width * lat_w, bytes_accessed=2 * emb * nseq * seq * width, transcendentals=0),
        name="mla_latents",
    )(h4, g_in, w_t, gains)


def solution(mesh):
    emb_count = mesh.shape["emb"]
    in_specs = (P("dp", None, "emb"), P("emb"), P("emb", "head"), P("head"), P("emb", "head"), P("head"), P("emb", None), P(None, "head", None), P(None, "head", None), P(None, "head", None), P("head", None, "emb"))
    out_specs = (P("dp", None, "emb"), P("dp", None, "head"), P("dp", None, None))

    def local_block(hidden, g_in, w_dq, g_q, w_dkv, g_kv, w_kr, w_uq, w_uk, w_uv, w_o):
        batch, seq, width = hidden.shape
        nope, rope = w_uk.shape[2], w_kr.shape[1]
        heads = w_uq.shape[1]
        cq_w, ckv_w = w_dq.shape[1], w_dkv.shape[1]
        scale = MSCALE * MSCALE / math.sqrt(w_uq.shape[2])
        w_t = jnp.concatenate([w_dq.T, w_dkv.T, w_kr.T, w_kr.T], axis=0)
        g_loc = jnp.concatenate([g_q, g_kv]).reshape(2, 2 * rope)
        gains = jnp.pad(g_loc, ((0, seq // (batch // emb_count) - 2), (0, 0)))
        h4 = hidden.reshape(emb_count, batch // emb_count, seq, width)
        lat, own = latents(h4, g_in[None], w_t, gains, cq_w, ckv_w, rope)
        weights = (
            w_uq.transpose(1, 2, 0).reshape(-1, w_uq.shape[0]),
            w_uk.reshape(w_uk.shape[0], heads * nope),
            w_uv.reshape(w_uv.shape[0], -1),
        )
        o, small = attention(lat, own, weights, g_kv[None], rope_rows(seq, rope), scale, heads, rope, cq_w)
        small_all = lax.all_gather(small, "emb", axis=0, tiled=True)
        result = tail(o, w_o.reshape(-1, w_o.shape[2]), hidden, emb_count)
        return result, small_all[..., :ckv_w], small_all[..., ckv_w:]

    return jax.shard_map(local_block, mesh=mesh, in_specs=in_specs, out_specs=out_specs, check_vma=False)
```

time: 1470 us -> 472 us (0.32)
  matrix products: 630 us -> 0 us
  waiting for transfers between devices: 567 us -> 0.08 us
  Pallas kernels: 0 us -> 419 us
  other arithmetic: 93.8 us -> 3.33 us
  local copies, waits for them, and re-layouts: 103 us -> 34.6 us
  loops' own time: 41 us -> 0 us
  blocking collectives: 16.1 us -> 0 us
    dot_general x323 -> x0, matrix products: 561 us -> none  [the longest x64 168 us: attend_block(): jnp.einsum('irl,ilw->irw', attn_prob, v_heads, preferred_element_type=jnp...]
    pallas_call x0 -> x3, Pallas kernels: none -> 419 us  [the longest x1 293 us: tail(): pl.pallas_call(functools.partial(tail_kernel, rows), out_shape=jax.ShapeD...]
    psum x3 -> x0, waiting for transfers between devices: 417 us -> none  [the longest x1 257 us: local_block(): attn_sum = lax.psum(attn_part, 'head')]
    all_gather x2 -> x1, waiting for transfers between devices: 150 us -> 0.02 us  [local_block(): small_all = lax.all_gather(small, 'emb', axis=0, tiled=True)]
    while x32 -> x0, matrix products: 69.5 us -> none
    another operation x33 -> x0, loops' own time: 41 us -> none  [the longest x32 38.9 us: causal_attention(): return lax.map(attend_block, jnp.arange(seq_len // q_block))]
    dynamic_slice x64 -> x0, local copies, waits for them, and re-layouts: 36.7 us -> none  [causal_attention(): return lax.map(attend_block, jnp.arange(seq_len // q_block))]
    convert_element_type x39 -> x0, other arithmetic: 36.6 us -> none  [the longest x1 28 us: local_block(): (hidden.astype(jnp.float32) + attn_sum.astype(jnp.float32)).astype(jnp.bf...]
  transfers between devices with their start and end apart: 5 -> 1, of which waited for: 5 -> 0; matrix products, arithmetic and copies ran while one was open for 1% -> 0% of each run, Pallas kernels for 0% -> 62%
where the time goes in v1:
time: 472 us; the launch traced here: 471 us
  Pallas kernels  419 us (89%)
  local copies, waits for them, and re-layouts  34.6 us (7%)
  between operations  14.1 us (3%)
    pallas_call x1, Pallas kernels, tail(): pl.pallas_call(functools.partial(tail_kernel, rows), out_shape=jax.ShapeD...  293 us
    pallas_call x1, Pallas kernels, latents(): pl.pallas_call(functools.partial(latent_kernel, cq_w, ckv_w, kr_w, width...  80.5 us
    pallas_call x1, Pallas kernels, attention(): pl.pallas_call(functools.partial(attn_kernel, heads, rope, cq_w, scale),...  46.1 us
    unnamed x9, local copies, waits for them, and re-layouts  24.8 us
  transfers between devices with their start and end apart: 1, of which 0 were waited for; matrix products, arithmetic and copies ran while one was open for 0% of the time, Pallas kernels for 62%

profile of v1, /device:TPU:97, one launch (start us, length us, event | category | flops | bytes accessed | tf_op | source)
XLA Modules:
  0.0 471.4 jit_solution(5422215451706529351)
XLA Ops:
  7.2 0.1 all-gather.2.cloned.1.call-start
  7.3 0.5 fusion.2
  7.8 1.3 broadcast_in_dim.8.g_ref
  9.1 0.7 maximum_bitcast_fusion
  9.8 0.6 pad.4.gains_ref
  10.4 0.0 copy-start
  10.4 0.0 copy-start.1
  10.4 0.0 copy-start.2
  10.4 3.5 copy_bitcast_fusion
  13.9 1.0 pad_maximum_fusion.1
  14.8 0.0 copy-done
  14.9 0.0 copy-done.1
  14.9 0.0 copy-done.2
  14.9 1.1 pad_maximum_fusion.w_ref
  16.0 80.5 %mla_latents.1 = (bf16[8,8,288,256]{3,2,1,0:T(8,128)(2,1)}, bf16[8,288,256]{2,1,0:T(8,128)(2,1)}) custom-call(bf16[4,8,256,1536]{3,2,1,0:T(8,128)(2,1)} %bitcast.19, bf16[1,1536]{1,0:T(2,128)(2,1)} %broadcast_in_dim.8.g_ref, bf16[384,1536]{1,0:T(8,128)(2,1)} %pad_maximum_fusion.w_ref, bf16[32,128]{1,0:T(8,128)(2,1)} %pad.4.gains_ref), custom_call_target="tpu_custom_call" | custom-call | flops 6442450944 | bytes 25165824 | tf_op jit(solution)/shard_map/mla_latents/pallas_call | solution.py:530
  96.5 46.1 %mla_attention.1 = (bf16[8,256,1024]{2,1,0:T(8,128)(2,1)}, bf16[8,256,128]{2,1,0:T(8,128)(2,1)}) custom-call(bf16[8,8,288,256]{3,2,1,0:T(8,128)(2,1)} %get-tuple-element.7.lat_ref, bf16[8,288,256]{2,1,0:T(8,128)(2,1)} %get-tuple-element.8.own_ref, bf16[1536,1536]{1,0:T(8,128)(2,1)} %bitcast.26, bf16[512,1024]{1,0:T(8,128)(2,1)} %get-tuple-element.25.wk_ref, ...), custom_call_target="tpu_custom_call" | custom-call | flops 18253611008 | bytes 9437184 | tf_op jit(solution)/shard_map/mla_attention/pallas_call | solution.py:101
  142.5 0.1 all-gather.2.cloned.1.call-update
  142.6 292.7 %mla_tail.1 = bf16[4,8,256,1536]{3,2,1,0:T(8,128)(2,1)} custom-call(bf16[8,256,1024]{2,1,0:T(8,128)(2,1)} %get-tuple-element.9.o_hbm, bf16[1024,1536]{1,0:T(8,128)(2,1)} %bitcast.27, bf16[4,8,256,1536]{3,2,1,0:T(8,128)(2,1)} %bitcast.20), custom_call_target="tpu_custom_call" | custom-call | flops 25769803776 | bytes 50331648 | tf_op jit(solution)/shard_map/mla_tail/pallas_call | solution.py:326
  435.3 0.0 all-gather.2.cloned.1.call-done
  435.4 4.4 fusion.3
  439.8 2.7 copy.16
  442.5 1.6 copy.17
  444.1 20.5 %copy.23 = bf16[32,256,1536]{2,1,0:T(8,128)(2,1)} copy(bf16[32,256,1536]{2,1,0:T(8,128)(2,1)} %bitcast.18) | data formatting | bytes 50331648
  (1 shorter events, 0.0 us)
Async XLA Ops:
  7.2 428.2 %all-gather.2.cloned.1.call-start = ((), (), s32[]{:S(2)}) async-start(), calls=%async_computation | async-start | bytes 2621440 | tf_op jit(solution)/shard_map/all_gather | solution.py:578
  10.4 4.4 copy-start
  10.4 4.4 copy-start.1
  10.4 4.4 copy-start.2
Sparse Core Ops, SparseCore 0:
  142.7 43.9 all-gather.1

commit v2 on v1

--- a/solution.py
+++ b/solution.py
@@ -52,7 +52,7 @@
     own = own_ref[0, :seq].astype(F32)
     own_ckv = (own[:, cq_w:] * rkv * gown_ref[...].astype(F32)).astype(BF16)
     kpe2 = rot(jnp.concatenate([lat_ref[j, 0, seq:, : width // 2] for j in range(parts)], axis=0).astype(F32))
-    small_ref[0] = jnp.concatenate([own_ckv, kpe2[:, :rope]], axis=-1)
+    small_ref[0] = jnp.concatenate([own_ckv, kpe2[:, :rope]], axis=-1).astype(F32).T.astype(BF16)
     zero = jnp.zeros_like(kpe2)
     kpe = (jnp.where(lane < rope, kpe2, zero), jnp.where(lane >= rope, kpe2, zero))
 
@@ -102,8 +102,8 @@
         functools.partial(attn_kernel, heads, rope, cq_w, scale),
         grid=(nseq,),
         in_specs=[pl.BlockSpec((parts, 1, ext, width), lambda s: (0, s, 0, 0)), pl.BlockSpec((1, ext, width), lambda s: (s, 0, 0))] + [whole(a) for a in (*weights, gown, *tables)],
-        out_specs=[pl.BlockSpec((1, seq, o_w), lambda s: (s, 0, 0)), pl.BlockSpec((1, seq, 2 * rope), lambda s: (s, 0, 0))],
-        out_shape=[jax.ShapeDtypeStruct((nseq, seq, o_w), BF16), jax.ShapeDtypeStruct((nseq, seq, 2 * rope), BF16)],
+        out_specs=[pl.BlockSpec((1, seq, o_w), lambda s: (s, 0, 0)), pl.BlockSpec((1, 2 * rope, seq), lambda s: (s, 0, 0))],
+        out_shape=[jax.ShapeDtypeStruct((nseq, seq, o_w), BF16), jax.ShapeDtypeStruct((nseq, 2 * rope, seq), BF16)],
         compiler_params=pltpu.CompilerParams(vmem_limit_bytes=60 * 1024 * 1024),
         cost_estimate=pl.CostEstimate(flops=flops, bytes_accessed=lat.size * 2, transcendentals=0),
         name="mla_attention",
@@ -113,7 +113,7 @@
 MESH = pl.DeviceIdType.MESH
 
 
-def tail_kernel(rows, o_hbm, w_ref, h_hbm, out_hbm, obuf, pall, precv, r2p, r2m, r1p, r1m, fin, hbuf, osend, orecv, hsend, hrecv, loc, s_snd, s_rcv, x_snd, x_rcv, g_snd, g_rcv, q_snd, q_rcv):
+def tail_kernel(rows, o_hbm, w_ref, h_hbm, sm_hbm, out_hbm, smo_hbm, sbuf, sm_loc, sm_snd, sm_rcv, obuf, pall, precv, r2p, r2m, r1p, r1m, fin, hbuf, osend, orecv, hsend, hrecv, loc, s_snd, s_rcv, x_snd, x_rcv, g_snd, g_rcv, q_snd, q_rcv):
     y, j = lax.axis_index("emb"), lax.axis_index("head")
     emb, nown, seq, width = out_hbm.shape
     ring = nown // 2
@@ -126,11 +126,12 @@
     y_next, y_prev = (y + 1) % emb, (y + emb - 1) % emb
     to_next, to_prev = {"head": 2 * x_next + c}, {"head": 2 * x_prev + c}
     to_sib = {"head": 2 * x + 1 - c}
-    to_up, to_down = {"emb": y_next}, {"emb": y_prev}
+    to_up, to_down, to_opp = {"emb": y_next}, {"emb": y_prev}, {"emb": (y + 2) % emb}
+    lead = quarters // 2
     half_k = nown // 2
 
     barrier = pltpu.get_barrier_semaphore()
-    for dev in (to_next, to_prev, to_sib, to_up, to_down):
+    for dev in (to_next, to_prev, to_sib, to_up, to_down, to_opp):
         pl.semaphore_signal(barrier, inc=1, device_id=dev, device_id_type=MESH)
 
     def remote(src, dst, ssem, rsem, dev):
@@ -142,8 +143,16 @@
     h_in = pltpu.make_async_copy(h_hbm.at[:, j], hbuf, loc.at[quarters])
     for r in range(quarters):
         own_in(r).start()
+    sm_in = pltpu.make_async_copy(sm_hbm, sbuf, sm_loc.at[0])
+    sm_own = pltpu.make_async_copy(sbuf, smo_hbm.at[y], sm_loc.at[1])
     h_in.start()
-    pl.semaphore_wait(barrier, 5)
+    sm_in.start()
+    pl.semaphore_wait(barrier, 6)
+
+    def sm_copy(k, dev):
+        return remote(sbuf, smo_hbm.at[y], sm_snd.at[k], sm_rcv.at[k], dev)
+
+    sm_copies = (sm_copy(0, to_up), sm_copy(1, to_down), sm_copy(2, to_opp))
 
     def o_down(r):
         return remote(obuf.at[r], obuf.at[quarters + 3 * r], osend.at[2 * r], orecv.at[2 * r], to_down)
@@ -159,9 +168,12 @@
 
     for r in range(quarters):
         own_in(r).wait()
-        o_down(r).start()
-        o_up(r).start()
+        if r < lead:
+            o_down(r).start()
+            o_up(r).start()
     h_in.wait()
+    sm_in.wait()
+    sm_own.start()
 
     def place(u):
         v = u - quarters
@@ -207,16 +219,6 @@
         def _():
             v = u - quarters
             r = v // 3
-
-            @pl.when(v % 3 == 0)
-            def _():
-                o_down(r).wait_recv()
-                o_half_down(r).start()
-
-            @pl.when(v % 3 == 1)
-            def _():
-                o_up(r).wait_recv()
-                o_half_up(r).start()
 
             @pl.when(v % 3 == 2)
             def _():
@@ -284,6 +286,32 @@
             @pl.when((t >= lag) & (t < units + lag))
             def _():
                 stage(t - lag)
+
+        ahead = t - (quarters - 1)
+
+        @pl.when((ahead >= 0) & (ahead % 3 == 0) & (ahead < 3 * quarters))
+        def _():
+            r = ahead // 3
+            o_down(r).wait_recv()
+            o_half_down(r).start()
+            o_up(r).wait_recv()
+            o_half_up(r).start()
+
+            @pl.when(r + lead < quarters)
+            def _():
+                o_down(r + lead).start()
+                o_up(r + lead).start()
+
+            @pl.when(r == quarters - 1)
+            def _():
+                for cp in sm_copies:
+                    cp.start()
+
+    for k, src in enumerate((y_prev, y_next, (y + 2) % emb)):
+        remote(sbuf, smo_hbm.at[src], sm_snd.at[k], sm_rcv.at[k], to_up).wait_recv()
+    for cp in sm_copies:
+        cp.wait_send()
+    sm_own.wait()
 
     @pl.loop(0, units)
     def _(u):
@@ -315,20 +343,22 @@
         o_half_down(r).wait_send()
 
 
-def tail(o, w_o, hidden, emb):
+def tail(o, w_o, hidden, small, emb):
     nseq, seq, depth = o.shape
     batch, _, width = hidden.shape
     assert batch == emb * nseq and emb == 4 and nseq == 8
-    rows = seq // 4
-    units = 4 * emb
+    parts = 4
+    rows = seq // parts
+    units = parts * emb
     dma = pltpu.SemaphoreType.DMA
     h4 = hidden.reshape(emb, nseq, seq, width)
-    out = pl.pallas_call(
+    out, small_all = pl.pallas_call(
         functools.partial(tail_kernel, rows),
-        out_shape=jax.ShapeDtypeStruct(h4.shape, BF16),
-        in_specs=[pl.BlockSpec(memory_space=pl.ANY), pl.BlockSpec(memory_space=pltpu.VMEM), pl.BlockSpec(memory_space=pl.ANY)],
-        out_specs=pl.BlockSpec(memory_space=pl.ANY),
+        out_shape=[jax.ShapeDtypeStruct(h4.shape, BF16), jax.ShapeDtypeStruct((emb,) + small.shape, BF16)],
+        in_specs=[pl.BlockSpec(memory_space=pl.ANY), pl.BlockSpec(memory_space=pltpu.VMEM), pl.BlockSpec(memory_space=pl.ANY), pl.BlockSpec(memory_space=pl.ANY)],
+        out_specs=[pl.BlockSpec(memory_space=pl.ANY), pl.BlockSpec(memory_space=pl.ANY)],
         scratch_shapes=[
+            pltpu.VMEM(small.shape, BF16), dma((2,)), dma((3,)), dma((3,)),
             pltpu.VMEM((units, nseq, rows, depth), BF16),
             pltpu.VMEM((4, nseq // 2, 2, rows, width), BF16),
             pltpu.VMEM((units, nseq // 2, rows, width), BF16),
@@ -338,7 +368,7 @@
             pltpu.VMEM((units, rows, width), BF16),
             pltpu.VMEM((units, rows, width), BF16),
             pltpu.VMEM((emb, seq, width), BF16),
-            dma((8,)), dma((8,)), dma((8,)), dma((8,)), dma((5,)),
+            dma((2 * parts,)), dma((2 * parts,)), dma((2 * parts,)), dma((2 * parts,)), dma((parts + 1,)),
             dma((units,)), dma((units,)),
             dma((4, units)), dma((4, units)),
             dma((4, units)), dma((3, units)),
@@ -347,8 +377,8 @@
         compiler_params=pltpu.CompilerParams(collective_id=0, has_side_effects=True, vmem_limit_bytes=63 * 1024 * 1024),
         cost_estimate=pl.CostEstimate(flops=2 * batch * seq * depth * width, bytes_accessed=4 * batch * seq * width, transcendentals=0),
         name="mla_tail",
-    )(o, w_o, h4)
-    return out.reshape(batch, seq, width)
+    )(o, w_o, h4, small)
+    return out.reshape(batch, seq, width), small_all.reshape(batch, small.shape[1], seq)
 
 
 def latent_kernel(cq_w, ckv_w, kr_w, full_width, h_hbm, g_ref, w_ref, gains_ref, lat_hbm, own_hbm, hbuf, ssum, peers, pall, r2p, r2m, r1p, r1m, fin, h_sem, p_snd, p_rcv, y_snd, y_rcv, g_snd, g_rcv, q_snd, q_rcv):
@@ -575,8 +605,7 @@
             w_uv.reshape(w_uv.shape[0], -1),
         )
         o, small = attention(lat, own, weights, g_kv[None], rope_rows(seq, rope), scale, heads, rope, cq_w)
-        small_all = lax.all_gather(small, "emb", axis=0, tiled=True)
-        result = tail(o, w_o.reshape(-1, w_o.shape[2]), hidden, emb_count)
-        return result, small_all[..., :ckv_w], small_all[..., ckv_w:]
+        result, small_all = tail(o, w_o.reshape(-1, w_o.shape[2]), hidden, small, emb_count)
+        return result, small_all[:, :ckv_w].transpose(0, 2, 1), small_all[:, ckv_w:].transpose(0, 2, 1)
 
     return jax.shard_map(local_block, mesh=mesh, in_specs=in_specs, out_specs=out_specs, check_vma=False)

time: 472 us -> 392 us (0.83)
  Pallas kernels: 419 us -> 359 us
  between operations: 14.1 us -> 0.67 us
  local copies, waits for them, and re-layouts: 34.6 us -> 27.3 us
    pallas_call x1, Pallas kernels: 293 us -> 232 us  [tail(): pl.pallas_call(functools.partial(tail_kernel, rows), out_shape=[jax.Shape...]
    unnamed x9 -> x5, local copies, waits for them, and re-layouts: 24.8 us -> 20.5 us
  transfers between devices with their start and end apart: 1 -> 0, of which waited for: 0 -> 0; matrix products, arithmetic and copies ran while one was open for 0% -> 0% of each run, Pallas kernels for 62% -> 0%
where the time goes in v2:
time: 392 us
  Pallas kernels  359 us (92%)
  local copies, waits for them, and re-layouts  27.3 us (7%)
  other arithmetic  4.87 us (1%)
    pallas_call x1, Pallas kernels, tail(): pl.pallas_call(functools.partial(tail_kernel, rows), out_shape=[jax.Shape...  232 us
    pallas_call x1, Pallas kernels, latents(): pl.pallas_call(functools.partial(latent_kernel, cq_w, ckv_w, kr_w, width...  80.5 us
    pallas_call x1, Pallas kernels, attention(): pl.pallas_call(functools.partial(attn_kernel, heads, rope, cq_w, scale),...  46.5 us
    unnamed x5, local copies, waits for them, and re-layouts  20.5 us

profile of v2, /device:TPU:97, one launch (start us, length us, event | category | flops | bytes accessed | tf_op | source)
XLA Modules:
  0.0 391.6 jit_solution(6233456592007967237)
XLA Ops:
  0.6 0.0 copy-start
  0.6 0.0 copy-start.1
  0.7 0.9 maximum_bitcast_fusion
  1.6 1.3 broadcast_in_dim.8.g_ref
  2.8 0.6 pad.4.gains_ref
  3.4 0.5 fusion.2
  4.0 1.0 pad_maximum_fusion.1
  5.0 2.4 pad_maximum_fusion.w_ref
  7.4 0.0 copy-done
  7.4 0.0 copy-done.1
  7.4 1.8 copy_bitcast_fusion
  9.3 80.5 %mla_latents.1 = (bf16[8,8,288,256]{3,2,1,0:T(8,128)(2,1)}, bf16[8,288,256]{2,1,0:T(8,128)(2,1)}) custom-call(bf16[4,8,256,1536]{3,2,1,0:T(8,128)(2,1)} %bitcast.24, bf16[1,1536]{1,0:T(2,128)(2,1)} %broadcast_in_dim.8.g_ref, bf16[384,1536]{1,0:T(8,128)(2,1)} %pad_maximum_fusion.w_ref, bf16[32,128]{1,0:T(8,128)(2,1)} %pad.4.gains_ref), custom_call_target="tpu_custom_call" | custom-call | flops 6442450944 | bytes 25165824 | tf_op jit(solution)/shard_map/mla_latents/pallas_call | solution.py:560
  89.8 46.5 %mla_attention.1 = (bf16[8,256,1024]{2,1,0:T(8,128)(2,1)}, bf16[8,128,256]{2,1,0:T(8,128)(2,1)}) custom-call(bf16[8,8,288,256]{3,2,1,0:T(8,128)(2,1)} %get-tuple-element.9.lat_ref, bf16[8,288,256]{2,1,0:T(8,128)(2,1)} %get-tuple-element.10.own_ref, bf16[1536,1536]{1,0:T(8,128)(2,1)} %bitcast.32, bf16[512,1024]{1,0:T(8,128)(2,1)} %get-tuple-element.23.wk_ref, ...), custom_call_target="tpu_custom_call" | custom-call | flops 18253611008 | bytes 9437184 | tf_op jit(solution)/shard_map/mla_attention/pallas_call | solution.py:101
  136.3 231.7 %mla_tail.1 = (bf16[4,8,256,1536]{3,2,1,0:T(8,128)(2,1)}, bf16[4,8,128,256]{3,2,1,0:T(8,128)(2,1)}) custom-call(bf16[8,256,1024]{2,1,0:T(8,128)(2,1)} %get-tuple-element.11.o_hbm, bf16[1024,1536]{1,0:T(8,128)(2,1)} %bitcast.33, bf16[4,8,256,1536]{3,2,1,0:T(8,128)(2,1)} %bitcast.25, bf16[8,128,256]{2,1,0:T(8,128)(2,1)} %get-tuple-element.12.sm_hbm), custom_call_target="tpu_custom_call" | custom-call | flops 25769803776 | bytes 50331648 | tf_op jit(solution)/shard_map/mla_tail/pallas_call | solution.py:355
  368.0 3.1 slice_bitcast_fusion
  371.1 20.5 %copy.19 = bf16[32,256,1536]{2,1,0:T(8,128)(2,1)} copy(bf16[32,256,1536]{2,1,0:T(8,128)(2,1)} %bitcast.23) | data formatting | bytes 50331648
  (1 shorter events, 0.0 us)
Async XLA Ops:
  0.6 6.8 %copy-start = (bf16[512,8,128]{2,1,0:T(8,128)(2,1)S(1)}, bf16[512,8,128]{2,1,0:T(8,128)(2,1)}, u32[]{:S(2)}) copy-start(bf16[512,8,128]{2,1,0:T(8,128)(2,1)} %param.20) | copy-start | bytes 3145732
  0.6 6.8 %copy-start.1 = (bf16[512,8,128]{2,1,0:T(8,128)(2,1)S(1)}, bf16[512,8,128]{2,1,0:T(8,128)(2,1)}, u32[]{:S(2)}) copy-start(bf16[512,8,128]{2,1,0:T(8,128)(2,1)} %param.19) | copy-start | bytes 3145732
